TPU v7x, 32 devices: a whole 2x2x4 slice. The times are simulated.
32 devices in a mesh: gx: 4 (over y, core), gy: 4 (over z), gz: 2 (over x).
Axes of the slice: x: 2, y: 2, z: 4, core: 2. Of those that a mesh axis runs over, the one named last changes fastest.
Arguments:
- a_vals: float32 [4, 8, 2, 6, 128, 128], P('gy', 'gx', 'gz'), may hold values from -0.25 to 0.25
- a_cols: int32 [4, 8, 2, 6], P('gy', 'gx', 'gz'), may hold values from 0 to 15, as said below
- a_count: int32 [4, 8, 2], P('gy', 'gx', 'gz'), may hold values from 1 to 6, as said below
- p_vals: float32 [2, 16, 4, 1, 128, 128], P('gz', 'gy', 'gx'), may hold values from -6 to 6
- p_cols: int32 [2, 16, 4, 1], P('gz', 'gy', 'gx'), may hold values from 0 to 1, as said below
- p_count: int32 [2, 16, 4], P('gz', 'gy', 'gx'), may hold values from 0 to 1, as said below
Outputs:
- c_tiles: float32 [4096, 1024], P(('gy', 'gz'), 'gx')
Inputs may be any that keep to these rules, and one draw needn't show every extreme that they name: `a_cols`: inner tile indices of one block row and slice are distinct across its 6 slots. Slots 0 to a_count - 1 are live; the block rows of every device include one with all 6 slots live. `p_cols`: column tiles of one block row and group are distinct across its 1 slots. Slots 0 to p_count - 1 are live; the block rows of every device include one with all 1 slots live.
All inputs are finite; a program needn't handle non-finite values.
Results may differ from a plain program's by a relative error of at most 0.0003.
Values sent between devices are 32-bit elements; how exact they have to be, the bound alone decides.
A program may use at most 128 MiB of HBM per device.

v0:
```python
import jax
import jax.numpy as jnp
from jax import lax
from jax.sharding import PartitionSpec as P

COLS_DEV = 2
HIGHEST = lax.Precision.HIGHEST


def placement_weights(counts, columns, column_tiles):
    slot_total = columns.shape[-1]
    alive_slots = jnp.arange(slot_total, dtype=jnp.int32) < counts[..., None]
    matches = columns[..., None] == jnp.arange(column_tiles, dtype=jnp.int32)
    return (alive_slots[..., None] & matches).astype(jnp.float32)


def body(a_vals, a_cols, a_count, p_vals, p_cols, p_count):
    tile_size = a_vals.shape[-1]
    slots_a = a_vals.shape[3]
    alive_a = jnp.arange(slots_a, dtype=jnp.int32) < a_count[..., None]
    a_masked = jnp.where(alive_a[..., None, None], a_vals, 0.0)
    weights = placement_weights(p_count, p_cols, COLS_DEV)
    strip_width = COLS_DEV * tile_size
    values_all, weights_all = (
        lax.all_gather(p_vals, "gy", axis=1, tiled=True),
        lax.all_gather(weights, "gy", axis=1, tiled=True),
    )
    values_all = values_all[0, :, 0]
    weights_all = weights_all[0, :, 0]
    tile_part = lax.all_gather(a_masked, "gx", axis=1, tiled=True)
    columns = lax.all_gather(a_cols, "gx", axis=1, tiled=True)
    row_count = tile_part.shape[1]
    block_tile_part = tile_part[0, :, 0]
    indices = columns[0, :, 0]
    chosen = values_all[indices]
    product = jnp.einsum("nsij,nspjk->nspik", block_tile_part, chosen, precision=HIGHEST)
    placed = jnp.einsum("nspc,nspik->nick", weights_all[indices], product, precision=HIGHEST)
    block = placed.reshape(placed.shape[0], tile_size, strip_width).reshape(
        row_count * tile_size, strip_width
    )
    return lax.psum_scatter(block, "gz", scatter_dimension=0, tiled=True)


def solution(mesh):
    placed = (
        P("gy", "gx", "gz", None, None, None),
        P("gy", "gx", "gz", None),
        P("gy", "gx", "gz"),
        P("gz", "gy", "gx", None, None, None),
        P("gz", "gy", "gx", None),
        P("gz", "gy", "gx"),
    )
    return jax.shard_map(
        body, mesh=mesh, in_specs=placed, out_specs=P(("gy", "gz"), "gx"), check_vma=False
    )
```

profile of v0, /device:TPU:0, one launch (start us, length us, event | category | flops | bytes accessed | tf_op | source)
XLA Modules:
  0.0 114.0 jit_solution(6142502463794559515)
XLA Ops:
  6.5 0.7 all-gather.3.cloned.1.call-update
  7.3 0.0 all-gather.5.cloned.1.call-start
  7.3 0.7 iota_compare_fusion
  8.0 2.1 %bitcast_select_fusion = f32[1,2,1,6,128,128]{5,4,3,2,0,1:T(8,128)} fusion(f32[1,2,1,6,128,128]{5,4,3,2,1,0:T(8,128)} %param.6, pred[2,6]{1,0:T(4,128)(4,1)S(1)} %iota_compare_fusion), kind=kLoop, calls=%fused_computation.6 | loop fusion | flops 196608 | bytes 1572876 | tf_op jit(solution)/shard_map/jit(_where)/select_n | solution.py:21
  10.2 0.0 reduce-scatter.2.cloned.1.call-start
  10.2 0.7 compare_bitcast_fusion
  10.9 0.7 and_convert_fusion
  11.6 13.7 %all_gather.15 = f32[1,16,1,1,2]{4,3,2,0,1:T(1,128)S(1)} all-gather(f32[1,4,1,1,2]{4,3,2,0,1:T(1,128)S(1)} %and_convert_fusion), channel_id=1, replica_groups=mesh['gx'=4,'gy'=4,'gz'=2] {'gy'}, dimensions={1}, use_global_device_ids=true | all-gather | bytes 160 | tf_op jit(solution)/shard_map/all_gather | solution.py:26
  25.4 5.3 %all_gather.13 = s32[1,8,1,6]{3,2,0,1:T(1,128)S(1)} all-gather(s32[1,2,1,6]{3,2,0,1:T(1,128)} %bitcast.44), channel_id=1, replica_groups=mesh['gx'=4,'gy'=4,'gz'=2] {'gx'}, dimensions={1}, use_global_device_ids=true | all-gather | bytes 240 | tf_op jit(solution)/shard_map/all_gather | solution.py:31
  30.6 0.1 copy.25
  30.7 0.1 copy.26
  30.8 0.1 reshape.152
  30.9 0.6 gather_fusion.1
  31.5 0.1 copy.31
  31.6 0.1 reshape.147
  31.6 8.1 %all-gather.3.cloned.1.call-done = f32[1,16,1,1,128,128]{5,4,3,2,0,1:T(8,128)} async-done(((f32[1,4,1,1,128,128]{5,4,3,2,0,1:T(8,128)}), f32[1,16,1,1,128,128]{5,4,3,2,0,1:T(8,128)}) %all-gather.3.cloned.1.call-update) | async-done | bytes 1048592 | tf_op jit(solution)/shard_map/all_gather | solution.py:25
  39.7 3.7 %gather_fusion = f32[48,128,128]{2,1,0:T(8,128)} fusion(f32[16,128,128]{2,1,0:T(8,128)} %bitcast.38, s32[1024]{0:T(1024)S(1)} %pad_clamp_fusion), kind=kCustom, calls=%fused_computation | custom fusion | bytes 6291648 | tf_op jit(solution)/shard_map/gather | solution.py:35
  43.4 25.8 %all-gather.5.cloned.1.call-done = f32[1,8,1,6,128,128]{5,4,3,2,0,1:T(8,128)} async-done(((f32[1,2,1,6,128,128]{5,4,3,2,0,1:T(8,128)}), f32[1,8,1,6,128,128]{5,4,3,2,0,1:T(8,128)}) %all-gather.5.cloned.1.call-update) | async-done | bytes 3145744 | tf_op jit(solution)/shard_map/all_gather | solution.py:30
  69.1 7.2 %fusion.2 = f32[8,6,128,128]{2,3,1,0:T(8,128)S(1)} fusion(f32[8,6,128,128]{3,2,1,0:T(8,128)} %bitcast.37, f32[1,8,1,6,128,128]{5,4,3,2,0,1:T(8,128)} %all-gather.5.cloned.1.call-done), kind=kOutput, calls=%fused_computation.4 | convolution fusion | flops 1207959552 | bytes 9437184 | tf_op jit(solution)/shard_map/nsij,nspjk->nspik/dot_general | solution.py:36
  76.4 3.6 %copy.32 = f32[8,6,128,128]{3,1,2,0:T(8,128)} copy(f32[8,6,128,128]{2,3,1,0:T(8,128)S(1)} %fusion.2) | data formatting | bytes 6291456 | tf_op jit(solution)/shard_map/reshape.8
  80.0 5.9 %fusion.5 = f32[8,128,128,2]{2,3,1,0:T(2,128)S(1)} fusion(f32[8,6,128,128]{3,1,2,0:T(8,128)} %copy.32, f32[8,6,2,1]{1,0,2,3:T(8,128)S(1)} %bitcast.43), kind=kOutput, calls=%fused_computation.8 | convolution fusion | flops 18874368 | bytes 4194688 | tf_op jit(solution)/shard_map/nspc,nspik->nick/dot_general | solution.py:37
  85.9 1.0 copy.43
  86.9 0.0 reduce-scatter.2.cloned.1.call-update
  86.9 20.5 %reduce-scatter.2.cloned.1.call-done = f32[512,256]{1,0:T(8,128)} async-done(((f32[1024,256]{1,0:T(8,128)}), f32[512,256]{1,0:T(8,128)}) %reduce-scatter.2.cloned.1.call-update) | async-done | bytes 524304 | tf_op jit(solution)/shard_map/reduce_scatter | solution.py:41
  (4 shorter events, 0.0 us)
Async XLA Ops:
  6.5 33.2 %all-gather.3.cloned.1.call-start = ((), (), s32[]{:S(2)}) async-start(), calls=%async_computation.1 | async-start | bytes 1310720 | tf_op jit(solution)/shard_map/all_gather | solution.py:25
  7.3 61.9 %all-gather.5.cloned.1.call-start = ((), (), s32[]{:S(2)}) async-start(), calls=%async_computation.2 | async-start | bytes 3932160 | tf_op jit(solution)/shard_map/all_gather | solution.py:30
  10.2 97.3 %reduce-scatter.2.cloned.1.call-start = ((), (), s32[]{:S(2)}) async-start(), calls=%async_computation.3 | async-start | bytes 1572864 | tf_op jit(solution)/shard_map/reduce_scatter | solution.py:41
Sparse Core Ops, SparseCore 0:
  8.9 30.7 all-gather.2
  41.3 27.8 all-gather.4
  87.1 20.3 reduce-scatter.1
where the time goes:
time: 114 us
  waiting for transfers between devices  55.1 us (48%)
  blocking collectives  19 us (17%)
  matrix products  13.1 us (11%)
  between operations  13.1 us (11%)
  local copies, waits for them, and re-layouts  9.29 us (8%)
  other arithmetic  4.27 us (4%)
    all_gather x1, waiting for transfers between devices, body(): tile_part = lax.all_gather(a_masked, 'gx', axis=1, tiled=True)  25.8 us
    reduce_scatter x1, waiting for transfers between devices, body(): return lax.psum_scatter(block, 'gz', scatter_dimension=0, tiled=True)  20.5 us
    all_gather x1, blocking collectives, body(): lax.all_gather(weights, 'gy', axis=1, tiled=True)  13.7 us
    all_gather x1, waiting for transfers between devices, body(): lax.all_gather(p_vals, 'gy', axis=1, tiled=True)  8.07 us
    dot_general x1, matrix products, body(): jnp.einsum('nsij,nspjk->nspik', block_tile_part, chosen, precision=HIGHEST)  7.22 us
    dot_general x1, matrix products, body(): jnp.einsum('nspc,nspik->nick', weights_all[indices], product, precision=H...  5.89 us
    all_gather x1, blocking collectives, body(): columns = lax.all_gather(a_cols, 'gx', axis=1, tiled=True)  5.26 us
    another operation x2, local copies, waits for them, and re-layouts  3.69 us
  transfers between devices with their start and end apart: 3, of which 3 were waited for; matrix products, arithmetic and copies ran while one was open for 8% of the time, Pallas kernels for 0%

commit v1 on v0

--- a/solution.py
+++ b/solution.py
@@ -5,6 +5,17 @@
 
 COLS_DEV = 2
 HIGHEST = lax.Precision.HIGHEST
+
+
+def pass_along(shard, mesh_axis, dim):
+    size = lax.axis_size(mesh_axis)
+    right = [(i, (i + 1) % size) for i in range(size)]
+    parts = [shard]
+    for far in range(1, size):
+        parts = [lax.ppermute(parts[0], mesh_axis, right), *parts]
+    result = jnp.concatenate(parts, axis=dim)
+    shift = (lax.axis_index(mesh_axis) + 1) * parts[-1].shape[dim]
+    return jnp.roll(result, shift, axis=dim)
 
 
 def placement_weights(counts, columns, column_tiles):
@@ -27,7 +38,7 @@
     )
     values_all = values_all[0, :, 0]
     weights_all = weights_all[0, :, 0]
-    tile_part = lax.all_gather(a_masked, "gx", axis=1, tiled=True)
+    tile_part = pass_along(a_masked, "gx", 1)
     columns = lax.all_gather(a_cols, "gx", axis=1, tiled=True)
     row_count = tile_part.shape[1]
     block_tile_part = tile_part[0, :, 0]

time: 114 us -> 102 us (0.89)
  waiting for transfers between devices: 55.1 us -> 43.2 us
  matrix products: 13.1 us -> 11 us
  local copies, waits for them, and re-layouts: 9.29 us -> 10.8 us
    all_gather x1 -> x0, waiting for transfers between devices: 25.8 us -> none  [body(): tile_part = lax.all_gather(a_masked, 'gx', axis=1, tiled=True)]
    ppermute x0 -> x3, waiting for transfers between devices: none -> 23 us  [pass_along(): parts = [lax.ppermute(parts[0], mesh_axis, right), *parts]]
    all_gather x1, waiting for transfers between devices: 8.07 us -> 0.01 us  [body(): lax.all_gather(p_vals, 'gy', axis=1, tiled=True)]
    dot_general x1, matrix products: 7.22 us -> 5.13 us  [body(): jnp.einsum('nsij,nspjk->nspik', block_tile_part, chosen, precision=HIGHEST)]
    unnamed x1 -> x11, local copies, waits for them, and re-layouts: 1.04 us -> 2.62 us
  transfers between devices with their start and end apart: 3 -> 5, of which waited for: 3 -> 3; matrix products, arithmetic and copies ran while one was open for 8% -> 6% of each run, Pallas kernels for 0% -> 0%
where the time goes in v1:
time: 102 us
  waiting for transfers between devices  43.2 us (42%)
  blocking collectives  18.7 us (18%)
  between operations  13.5 us (13%)
  matrix products  11 us (11%)
  local copies, waits for them, and re-layouts  10.8 us (11%)
  other arithmetic  3.69 us (4%)
    ppermute x3, waiting for transfers between devices, pass_along(): parts = [lax.ppermute(parts[0], mesh_axis, right), *parts]  23 us
    reduce_scatter x1, waiting for transfers between devices, body(): return lax.psum_scatter(block, 'gz', scatter_dimension=0, tiled=True)  20.2 us
    all_gather x1, blocking collectives, body(): lax.all_gather(weights, 'gy', axis=1, tiled=True)  13.4 us
    dot_general x1, matrix products, body(): jnp.einsum('nspc,nspik->nick', weights_all[indices], product, precision=H...  5.89 us
    all_gather x1, blocking collectives, body(): columns = lax.all_gather(a_cols, 'gx', axis=1, tiled=True)  5.26 us
    dot_general x1, matrix products, body(): jnp.einsum('nsij,nspjk->nspik', block_tile_part, chosen, precision=HIGHEST)  5.13 us
    another operation x2, local copies, waits for them, and re-layouts  3.68 us
    gather x1, local copies, waits for them, and re-layouts, body(): chosen = values_all[indices]  3.63 us
  transfers between devices with their start and end apart: 5, of which 3 were waited for; matrix products, arithmetic and copies ran while one was open for 6% of the time, Pallas kernels for 0%

profile of v1, /device:TPU:0, one launch (start us, length us, event | category | flops | bytes accessed | tf_op | source)
XLA Modules:
  0.0 101.5 jit_solution(3817383681995379481)
XLA Ops:
  6.5 0.7 iota_compare_fusion
  7.3 1.3 %broadcast_select_fusion = f32[1,2,1,6,128,128]{5,4,3,2,1,0:T(8,128)S(1)} fusion(f32[1,2,1,6,128,128]{5,4,3,2,1,0:T(8,128)} %param.6, pred[2,6]{1,0:T(4,128)(4,1)S(1)} %iota_compare_fusion), kind=kLoop, calls=%fused_computation.7 | loop fusion | flops 196608 | bytes 1572876 | tf_op jit(solution)/shard_map/jit(_where)/select_n | solution.py:32
  8.6 0.5 collective-permute-start
  9.1 11.6 %collective-permute-done = f32[1,2,1,6,128,128]{5,4,3,2,1,0:T(8,128)S(1)} collective-permute-done((f32[1,2,1,6,128,128]{5,4,3,2,1,0:T(8,128)S(1)}, f32[1,2,1,6,128,128]{5,4,3,2,1,0:T(8,128)S(1)}, u32[]{:S(2)}, u32[]{:S(2)}) %collective-permute-start) | collective-permute-done | bytes 786464 | tf_op jit(solution)/shard_map/ppermute | solution.py:15
  20.8 11.3 %collective-permute-done.1 = f32[1,2,1,6,128,128]{5,4,3,2,1,0:T(8,128)S(1)} collective-permute-done((f32[1,2,1,6,128,128]{5,4,3,2,1,0:T(8,128)S(1)}, f32[1,2,1,6,128,128]{5,4,3,2,1,0:T(8,128)S(1)}, u32[]{:S(2)}, u32[]{:S(2)}) %collective-permute-start.1) | collective-permute-done | bytes 786464 | tf_op jit(solution)/shard_map/ppermute | solution.py:15
  32.2 0.7 compare_bitcast_fusion
  32.8 0.7 and_convert_fusion
  33.6 13.4 %all_gather.11 = f32[1,16,1,1,2]{4,3,2,0,1:T(1,128)S(1)} all-gather(f32[1,4,1,1,2]{4,3,2,0,1:T(1,128)S(1)} %and_convert_fusion), channel_id=1, replica_groups=mesh['gx'=4,'gy'=4,'gz'=2] {'gy'}, dimensions={1}, use_global_device_ids=true | all-gather | bytes 160 | tf_op jit(solution)/shard_map/all_gather | solution.py:37
  47.0 5.3 %all_gather.10 = s32[1,8,1,6]{3,2,0,1:T(1,128)S(1)} all-gather(s32[1,2,1,6]{3,2,0,1:T(1,128)} %bitcast.42), channel_id=1, replica_groups=mesh['gx'=4,'gy'=4,'gz'=2] {'gx'}, dimensions={1}, use_global_device_ids=true | all-gather | bytes 240 | tf_op jit(solution)/shard_map/all_gather | solution.py:42
  52.2 0.1 copy.23
  52.3 0.1 copy.24
  52.4 0.1 reshape.152
  52.5 0.6 gather_fusion.1
  53.1 0.1 copy.28
  53.2 0.1 reshape.147
  53.3 3.6 %gather_fusion = f32[48,128,128]{2,1,0:T(8,128)} fusion(f32[16,128,128]{2,1,0:T(8,128)} %bitcast.36, s32[1024]{0:T(1024)S(1)} %pad_clamp_fusion), kind=kCustom, calls=%fused_computation | custom fusion | bytes 6291648 | tf_op jit(solution)/shard_map/gather | solution.py:46
  57.1 0.1 constant_dynamic-update-slice_fusion.4
  57.5 0.1 constant_dynamic-update-slice_fusion
  57.6 1.2 %copy-done = f32[48,128,128]{2,1,0:T(8,128)S(1)} copy-done((f32[48,128,128]{2,1,0:T(8,128)S(1)}, f32[48,128,128]{2,1,0:T(8,128)}, u32[]{:S(2)}) %copy-start) | copy-done | bytes 3145752
  58.8 5.1 %fusion.3 = f32[8,6,128,128]{2,3,1,0:T(8,128)S(1)} fusion(f32[8,6,128,128]{3,2,1,0:T(8,128)S(1)} %bitcast.35, f32[1,16,1,6,128,128]{5,4,3,2,1,0:T(8,128)S(1)} %constant_dynamic-update-slice_fusion, s32[]{:T(128)S(6)} %select_n.31), kind=kOutput, calls=%fused_computation.5 | convolution fusion | flops 1207959552 | bytes 9437188 | tf_op jit(solution)/shard_map/nsij,nspjk->nspik/dot_general | solution.py:47
  63.9 3.6 %copy.29 = f32[8,6,128,128]{3,1,2,0:T(8,128)} copy(f32[8,6,128,128]{2,3,1,0:T(8,128)S(1)} %fusion.3) | data formatting | bytes 6291456 | tf_op jit(solution)/shard_map/reshape.8
  67.5 5.9 %fusion.6 = f32[8,128,128,2]{2,3,1,0:T(2,128)S(1)} fusion(f32[8,6,128,128]{3,1,2,0:T(8,128)} %copy.29, f32[8,6,2,1]{1,0,2,3:T(8,128)S(1)} %bitcast.41), kind=kOutput, calls=%fused_computation.17 | convolution fusion | flops 18874368 | bytes 4194688 | tf_op jit(solution)/shard_map/nspc,nspik->nick/dot_general | solution.py:48
  73.4 1.0 %copy.40 = f32[128,8,2,128]{3,1,2,0:T(8,128)} copy(f32[128,8,2,128]{3,2,1,0:T(2,128)S(1)} %bitcast.38) | data formatting | bytes 2097152
  74.5 20.2 %reduce-scatter.2.cloned.1.call-done = f32[512,256]{1,0:T(8,128)} async-done(((f32[1024,256]{1,0:T(8,128)}), f32[512,256]{1,0:T(8,128)}) %reduce-scatter.2.cloned.1.call-update) | async-done | bytes 524304 | tf_op jit(solution)/shard_map/reduce_scatter | solution.py:52
  (19 shorter events, 0.5 us)
Async XLA Ops:
  6.5 46.7 %all-gather.2.cloned.1.call-start = ((), (), s32[]{:S(2)}) async-start(), calls=%async_computation.1 | async-start | bytes 1310720 | tf_op jit(solution)/shard_map/all_gather | solution.py:36
  7.3 49.8 %copy-start.1 = (f32[1,2,1,6,128,128]{5,4,3,2,1,0:T(8,128)S(1)}, f32[1,2,1,6,128,128]{5,4,3,2,1,0:T(8,128)}, u32[]{:S(2)}) copy-start(f32[1,2,1,6,128,128]{5,4,3,2,1,0:T(8,128)} %param.6) | copy-start | bytes 2359300
  8.6 12.2 %collective-permute-start = (f32[1,2,1,6,128,128]{5,4,3,2,1,0:T(8,128)S(1)}, f32[1,2,1,6,128,128]{5,4,3,2,1,0:T(8,128)S(1)}, u32[]{:S(2)}, u32[]{:S(2)}) collective-permute-start(f32[1,2,1,6,128,128]{5,4,3,2,1,0:T(8,128)S(1)} %broadcast_select_fusion), channel_id=1, source_target_pairs={{0,8},{8,16},{16,24},{24,0},{1,9},{9,17},{17,25},{25,1},{2,10},{10... | collective-permute-start | bytes 2359304 | tf_op jit(solution)/shard_map/ppermute | solution.py:15
  20.8 11.4 %collective-permute-start.1 = (f32[1,2,1,6,128,128]{5,4,3,2,1,0:T(8,128)S(1)}, f32[1,2,1,6,128,128]{5,4,3,2,1,0:T(8,128)S(1)}, u32[]{:S(2)}, u32[]{:S(2)}) collective-permute-start(f32[1,2,1,6,128,128]{5,4,3,2,1,0:T(8,128)S(1)} %collective-permute-done), channel_id=1, source_target_pairs={{0,8},{8,16},{16,24},{24,0},{1,9},{9,17},{17,25},{25,1},{2,10},{10... | collective-permute-start | bytes 2359304 | tf_op jit(solution)/shard_map/ppermute | solution.py:15
  20.8 73.9 %reduce-scatter.2.cloned.1.call-start = ((), (), s32[]{:S(2)}) async-start(), calls=%async_computation.2 | async-start | bytes 1572864 | tf_op jit(solution)/shard_map/reduce_scatter | solution.py:52
  32.2 24.7 %collective-permute-start.2 = (f32[1,2,1,6,128,128]{5,4,3,2,1,0:T(8,128)S(1)}, f32[1,2,1,6,128,128]{5,4,3,2,1,0:T(8,128)S(1)}, u32[]{:S(2)}, u32[]{:S(2)}) collective-permute-start(f32[1,2,1,6,128,128]{5,4,3,2,1,0:T(8,128)S(1)} %collective-permute-done.1), channel_id=1, source_target_pairs={{0,8},{8,16},{16,24},{24,0},{1,9},{9,17},{17,25},{25,1},{2,10},{10... | collective-permute-start | bytes 2359304 | tf_op jit(solution)/shard_map/ppermute | solution.py:15
  56.9 1.9 %copy-start = (f32[48,128,128]{2,1,0:T(8,128)S(1)}, f32[48,128,128]{2,1,0:T(8,128)}, u32[]{:S(2)}) copy-start(f32[48,128,128]{2,1,0:T(8,128)} %gather_fusion) | copy-start | bytes 9437188
Sparse Core Ops, SparseCore 0:
  20.9 30.4 all-gather.1
  74.6 20.0 reduce-scatter.1
